TPU v7x, 256 devices: a whole 4x4x8 slice. The times are simulated.
256 devices in a mesh: row: 8 (over y, z_hi), col: 32 (over x, z_lo, core).
Axes of the slice: x: 4, y: 4, z: 8 (z_hi: 2, z_lo: 4; z = z_hi * 4 + z_lo), core: 2. Of those that a mesh axis runs over, the one named last changes fastest.
Arguments:
- pair_grad: float32 [2048, 2048, 128], P('row', 'col'), may hold values from -4 to 4
- out_weight: bfloat16 [1024, 128], replicated, may hold values from -0.1875 to 0.1875
- left_factor: bfloat16 [32, 32, 2048], P('col', None, 'row'), may hold values from -6 to 6
- right_factor: bfloat16 [32, 32, 2048], P('row', None, 'col'), may hold values from -6 to 6
Outputs:
- left_grad: float32 [32, 32, 2048], P('col', None, 'row')
- right_grad: float32 [32, 32, 2048], P('row', None, 'col')
All inputs are finite; a program needn't handle non-finite values.
Results may differ from a plain program's by a relative error of at most 0.0042.
Values may be sent and summed in bfloat16 or wider, within the bound.
A program may use at most 128 MiB of HBM per device.

v0:
```python
import jax
import jax.numpy as jnp
from jax import lax
from jax.sharding import PartitionSpec as P


def laid_out(blocks, dim):
    shape = list(blocks.shape[1:])
    shape[dim] *= blocks.shape[0]
    return jnp.moveaxis(blocks, 0, dim).reshape(shape)


def from_everyone(shard, axis):
    size = lax.axis_size(axis)
    return lax.all_to_all(
        jnp.broadcast_to(shard[None], (size, *shard.shape)), axis, 0, 0, tiled=True
    )


def gather_directly(shard, axis, dim):
    return laid_out(from_everyone(shard, axis), dim)


def split_up(shard, dim, size):
    shape = shard.shape
    blocks = shard.reshape(*shape[:dim], size, shape[dim] // size, *shape[dim + 1 :])
    return jnp.moveaxis(blocks, dim, 0)


def summed_on_arrival(shard, axis, dim):
    size = lax.axis_size(axis)
    blocks = lax.all_to_all(split_up(shard, dim, size), axis, 0, 0, tiled=True)
    return jnp.sum(blocks.astype(jnp.float32), axis=0)


def body(pair_grad, out_weight, left_factor, right_factor):
    first_row_span, second_row_span, pair_width = pair_grad.shape
    hidden_width = left_factor.shape[1]
    left_gathered = gather_directly(left_factor, "col", 0)
    right_all = gather_directly(right_factor, "row", 0)
    alignment_rows = left_gathered.shape[0]
    scale_factor_term = 1.0 / alignment_rows
    pair_low = pair_grad.astype(jnp.bfloat16)
    grid = out_weight.reshape(hidden_width, hidden_width, pair_width)
    wide = jnp.einsum("ijk,xyk->ijxy", pair_low, grid, preferred_element_type=jnp.float32)
    expanded = wide.astype(jnp.bfloat16)
    piece = right_all
    left_grad = summed_on_arrival(
        (
            jnp.einsum("ijxy,syj->sxi", expanded, piece, preferred_element_type=jnp.float32)
            * scale_factor_term
        ).astype(jnp.bfloat16),
        "col",
        0,
    )
    piece = left_gathered
    right_grad = summed_on_arrival(
        (
            jnp.einsum("ijxy,sxi->syj", expanded, piece, preferred_element_type=jnp.float32)
            * scale_factor_term
        ).astype(jnp.bfloat16),
        "row",
        0,
    )
    return (left_grad, right_grad)


def solution(mesh):
    placed = (P("row", "col", None), P(), P("col", None, "row"), P("row", None, "col"))
    return jax.shard_map(
        body,
        mesh=mesh,
        in_specs=placed,
        out_specs=(P("col", None, "row"), P("row", None, "col")),
        check_vma=False,
    )
```

profile of v0, /device:TPU:1, one launch (start us, length us, event | category | flops | bytes accessed | tf_op | source)
XLA Modules:
  0.0 123.0 jit_solution(10509454364107824942)
XLA Ops:
  0.6 0.0 copy-start
  0.6 0.8 copy.14
  1.5 0.1 broadcast_bitcast_fusion
  1.5 0.9 reshape.35
  2.4 11.6 %all-to-all-start = ((bf16[8,2,4096]{2,1,0:T(2,128)(2,1)}), bf16[8,2,4096]{2,1,0:T(2,128)(2,1)S(1)}, u32[]{:S(2)}, u32[]{:S(2)}) async-start(bf16[8,2,4096]{2,1,0:T(2,128)(2,1)} %reshape.35), calls=%async_computation | async-start | bytes 262144 | tf_op jit(solution)/shard_map/all_to_all | solution.py:15
  14.1 6.5 %convert_bitcast_fusion = bf16[256,64,128,1]{2,1,0,3:T(8,128)(2,1)} fusion(f32[256,64,128]{2,1,0:T(8,128)} %param.4), kind=kLoop, calls=%fused_computation.2 | loop fusion | flops 2097152 | bytes 12582912 | tf_op jit(solution)/shard_map/convert_element_type | solution.py:43
  20.6 2.9 %all-to-all-done = bf16[8,2,4096]{2,1,0:T(2,128)(2,1)S(1)} async-done(((bf16[8,2,4096]{2,1,0:T(2,128)(2,1)}), bf16[8,2,4096]{2,1,0:T(2,128)(2,1)S(1)}, u32[]{:S(2)}, u32[]{:S(2)}) %all-to-all-start) | async-done | bytes 131104 | tf_op jit(solution)/shard_map/all_to_all | solution.py:15
  23.5 1.6 %broadcast_in_dim.16 = bf16[32,1,32,256]{3,2,1,0:T(8,128)(2,1)} broadcast(bf16[32,256]{1,0:T(8,128)(2,1)} %bitcast.52), dimensions={2,3} | broadcast | bytes 540672 | tf_op jit(solution)/shard_map/broadcast_in_dim | solution.py:16
  25.1 7.9 %all-to-all-start.2 = ((bf16[32,1,32,256]{3,2,1,0:T(8,128)(2,1)}), bf16[32,1,32,256]{3,2,1,0:T(8,128)(2,1)S(1)}, u32[]{:S(2)}, u32[]{:S(2)}) async-start(bf16[32,1,32,256]{3,2,1,0:T(8,128)(2,1)} %broadcast_in_dim.16), calls=%async_computation.2 | async-start | bytes 1048576 | tf_op jit(solution)/shard_map/all_to_all | solution.py:15
  33.0 0.0 copy-done
  33.0 26.2 %convolution_convert_fusion = bf16[256,64,32,32]{0,3,2,1:T(8,128)(2,1)} fusion(bf16[32,32,128,1]{2,1,0,3:T(8,128)(2,1)S(1)} %bitcast.47, bf16[256,64,128,1]{2,1,0,3:T(8,128)(2,1)} %convert_bitcast_fusion), kind=kOutput, calls=%fused_computation | convolution fusion | flops 4311744512 | bytes 38010880 | tf_op jit(solution)/shard_map/ijk,xyk->ijxy/dot_general | solution.py:45
  59.2 0.2 reshape.36
  59.4 0.8 copy.15
  60.2 0.0 all-to-all-done.2
  60.2 15.1 %fusion.6 = bf16[32,32,64]{0,1,2:T(8,128)(2,1)S(1)} fusion(bf16[256,64,32,32]{0,3,2,1:T(8,128)(2,1)} %convolution_convert_fusion, bf16[32,1,32,256]{3,2,1,0:T(8,128)(2,1)S(1)} %all-to-all-done.2), kind=kOutput, calls=%fused_computation.10 | convolution fusion | flops 1073872896 | bytes 34209792 | tf_op jit(solution)/shard_map/ijxy,sxi->syj/dot_general | solution.py:59
  75.4 0.8 copy.18
  76.2 0.9 reshape.37
  77.1 5.3 %all-to-all-start.3 = ((bf16[8,2,4096]{2,1,0:T(2,128)(2,1)}), bf16[8,2,4096]{2,1,0:T(2,128)(2,1)S(1)}, u32[]{:S(2)}, u32[]{:S(2)}) async-start(bf16[8,2,4096]{2,1,0:T(2,128)(2,1)} %reshape.37), calls=%async_computation.3 | async-start | bytes 262144 | tf_op jit(solution)/shard_map/all_to_all | solution.py:32
  82.3 14.1 %fusion.5 = bf16[32,1,32,256]{3,0,2,1:T(8,128)(2,1)S(1)} fusion(bf16[32,32,64,1]{1,0,3,2:T(8,128)(2,1)S(1)} %bitcast.48, bf16[256,64,32,32]{0,3,2,1:T(8,128)(2,1)} %convolution_convert_fusion), kind=kOutput, calls=%fused_computation.9 | convolution fusion | flops 1074266112 | bytes 34209792 | tf_op jit(solution)/shard_map/ijxy,syj->sxi/dot_general | solution.py:50
  96.5 1.1 copy.16
  97.6 0.0 all-to-all-done.3
  97.6 8.0 %all-to-all-start.1 = ((bf16[32,1,32,256]{3,2,1,0:T(8,128)(2,1)}), bf16[32,1,32,256]{3,2,1,0:T(8,128)(2,1)S(1)}, u32[]{:S(2)}, u32[]{:S(2)}) async-start(bf16[32,1,32,256]{3,2,1,0:T(8,128)(2,1)} %copy.16), calls=%async_computation.1 | async-start | bytes 1048576 | tf_op jit(solution)/shard_map/all_to_all | solution.py:32
  105.6 0.2 reshape.38
  105.8 0.7 convert_reduce_fusion.1
  106.5 15.9 %all-to-all-done.1 = bf16[32,1,32,256]{3,2,1,0:T(8,128)(2,1)S(1)} async-done(((bf16[32,1,32,256]{3,2,1,0:T(8,128)(2,1)}), bf16[32,1,32,256]{3,2,1,0:T(8,128)(2,1)S(1)}, u32[]{:S(2)}, u32[]{:S(2)}) %all-to-all-start.1) | async-done | bytes 524320 | tf_op jit(solution)/shard_map/all_to_all | solution.py:32
  122.3 0.7 convert_reduce_fusion
Async XLA Ops:
  0.6 32.4 %copy-start = (bf16[1024,128]{1,0:T(8,128)(2,1)S(1)}, bf16[1024,128]{1,0:T(8,128)(2,1)}, u32[]{:S(2)}) copy-start(bf16[1024,128]{1,0:T(8,128)(2,1)} %param.5) | copy-start | bytes 786436
  2.4 21.1 %all-to-all-start = ((bf16[8,2,4096]{2,1,0:T(2,128)(2,1)}), bf16[8,2,4096]{2,1,0:T(2,128)(2,1)S(1)}, u32[]{:S(2)}, u32[]{:S(2)}) async-start(bf16[8,2,4096]{2,1,0:T(2,128)(2,1)} %reshape.35), calls=%async_computation | async-start | bytes 262144 | tf_op jit(solution)/shard_map/all_to_all | solution.py:15
  25.1 35.1 %all-to-all-start.2 = ((bf16[32,1,32,256]{3,2,1,0:T(8,128)(2,1)}), bf16[32,1,32,256]{3,2,1,0:T(8,128)(2,1)S(1)}, u32[]{:S(2)}, u32[]{:S(2)}) async-start(bf16[32,1,32,256]{3,2,1,0:T(8,128)(2,1)} %broadcast_in_dim.16), calls=%async_computation.2 | async-start | bytes 1048576 | tf_op jit(solution)/shard_map/all_to_all | solution.py:15
  77.1 20.5 %all-to-all-start.3 = ((bf16[8,2,4096]{2,1,0:T(2,128)(2,1)}), bf16[8,2,4096]{2,1,0:T(2,128)(2,1)S(1)}, u32[]{:S(2)}, u32[]{:S(2)}) async-start(bf16[8,2,4096]{2,1,0:T(2,128)(2,1)} %reshape.37), calls=%async_computation.3 | async-start | bytes 262144 | tf_op jit(solution)/shard_map/all_to_all | solution.py:32
  97.6 24.8 %all-to-all-start.1 = ((bf16[32,1,32,256]{3,2,1,0:T(8,128)(2,1)}), bf16[32,1,32,256]{3,2,1,0:T(8,128)(2,1)S(1)}, u32[]{:S(2)}, u32[]{:S(2)}) async-start(bf16[32,1,32,256]{3,2,1,0:T(8,128)(2,1)} %copy.16), calls=%async_computation.1 | async-start | bytes 1048576 | tf_op jit(solution)/shard_map/all_to_all | solution.py:32
where the time goes:
time: 124 us; the launch traced here: 123 us
  matrix products  55.5 us (45%)
  starting transfers between devices  32.8 us (26%)
  waiting for transfers between devices  18.8 us (15%)
  other arithmetic  7.92 us (6%)
  local copies, waits for them, and re-layouts  7.32 us (6%)
    dot_general x1, matrix products, body(): jnp.einsum('ijk,xyk->ijxy', pair_low, grid, preferred_element_type=jnp.fl...  26.2 us
    all_to_all x2, starting transfers between devices, from_everyone(): lax.all_to_all(jnp.broadcast_to(shard[None], (size, *shard.shape)), axis,...  19.6 us
    all_to_all x2, waiting for transfers between devices, summed_on_arrival(): blocks = lax.all_to_all(split_up(shard, dim, size), axis, 0, 0, tiled=True)  15.9 us
    dot_general x1, matrix products, body(): jnp.einsum('ijxy,sxi->syj', expanded, piece, preferred_element_type=jnp.f...  15.1 us
    dot_general x1, matrix products, body(): jnp.einsum('ijxy,syj->sxi', expanded, piece, preferred_element_type=jnp.f...  14.1 us
    all_to_all x2, starting transfers between devices, summed_on_arrival(): blocks = lax.all_to_all(split_up(shard, dim, size), axis, 0, 0, tiled=True)  13.2 us
    convert_element_type x1, other arithmetic, body(): pair_low = pair_grad.astype(jnp.bfloat16)  6.54 us
    unnamed x8, local copies, waits for them, and re-layouts  3.09 us
  transfers between devices with their start and end apart: 4, of which 2 were waited for; matrix products, arithmetic and copies ran while one was open for 41% of the time, Pallas kernels for 0%

commit v1 on v0

v1 whole, which is shorter than its diff:
```python
import jax
import jax.numpy as jnp
from jax import lax
from jax.experimental import pallas as pl
from jax.experimental.pallas import tpu as pltpu
from jax.sharding import PartitionSpec as P

f32, bf16 = jnp.float32, jnp.bfloat16
MESH = pl.DeviceIdType.MESH
NT = (((1,), (1,)), ((), ()))

I, J, K, X, Y, S = 256, 64, 128, 32, 32, 32
ROWS, COLS, CHIPS = 8, 32, 16
G = 4
JA = 16
SCALE = 1.0 / S


def kernel(
    pair, weight, left, right,
    left_out, right_out,
    pf, pb, abuf, ubuf,
    rmine, rin, rst, rbuf,
    lin, lst, lbuf,
    acc, lxs, lx, lsend, lr,
    rt, rsend, rr,
    psem, osem, rs_sem, rr_in, ls_sem, l_in, lrs_sem, lr_in,
    xs_sem, x_in, gs_sem, g_in, hs_sem, h_in,
):
    row, col = lax.axis_index("row"), lax.axis_index("col")
    y, zh = row // 2, row % 2
    chip, core = col // 2, col % 2
    mate = (row, chip * 2 + 1 - core)

    def row_peer(h, t):
        return ((y + t) % 4) * 2 + (zh + h) % 2

    def chip_peer(d):
        return ((chip + d) % CHIPS) * 2 + core

    def slot_of(s):
        owner, s4 = s // G, s % G
        return ((owner + zh) % 2) * 16 + (s4 % 2) * 8 + (s4 // 2) * 4 + (owner // 2 - y + 4) % 4

    mine = slot_of(col)

    own = pltpu.make_async_copy(left.at[0], lin.at[mine], osem)
    own.start()

    @pl.loop(0, I)
    def _(i):
        pltpu.make_async_copy(pair.at[i], pf.at[:, i, :], psem).start()

    barrier = pltpu.get_barrier_semaphore()
    for h in range(2):
        for t in range(4):
            if h or t:
                pl.semaphore_signal(barrier, inc=1, device_id=(row_peer(h, t), col), device_id_type=MESH)
    pl.semaphore_signal(barrier, inc=1, device_id=mate, device_id_type=MESH)

    @pl.loop(1, CHIPS)
    def _(d):
        pl.semaphore_signal(barrier, inc=1, device_id=(row, chip_peer(d)), device_id_type=MESH)

    flipped = jnp.transpose(right[...].reshape(G * Y, J).astype(f32)).astype(bf16)
    rmine[...] = flipped
    rin[0] = flipped
    own.wait()
    pl.semaphore_wait(barrier, ROWS - 1 + 1 + CHIPS - 1)

    def right_copy(h, t):
        return pltpu.make_async_remote_copy(
            rmine, rin.at[h * 4 + (4 - t) % 4], rs_sem, rr_in.at[h],
            device_id=(row_peer(h, t), col), device_id_type=MESH)

    for h in (1, 0):
        for t in range(4):
            if h or t:
                right_copy(h, t).start()

    @pl.loop(1, CHIPS)
    def _(d):
        pltpu.make_async_remote_copy(
            lin.at[mine], lin.at[mine], ls_sem, l_in,
            device_id=(row, chip_peer(d)), device_id_type=MESH).start()

    lane = lax.broadcasted_iota(jnp.int32, (4, 128), 1) // 32

    def spread_right(h):
        rst[pl.ds(4 * h, 4)] = rin[pl.ds(4 * h, 4)].astype(f32)

        @pl.loop(0, J // 4)
        def _(q):
            for e in range(4):
                v = rst[pl.ds(4 * h, 4), q * 4 + e, :]
                rows = [jnp.where(lane == s4, v, 0.0) for s4 in (0, 2, 1, 3)]
                rbuf[h, q * 4 + e] = jnp.concatenate(rows, axis=0).astype(bf16)

    def pair_of(x2):
        a = weight[pl.ds(64 * x2, 32), :]
        b = weight[pl.ds(64 * x2 + 32, 32), :]
        return jnp.concatenate([a, b], axis=1)

    def times_weight(h):
        @pl.loop(0, J // JA)
        def _(c):
            lhs = rbuf[h, pl.ds(c * JA, JA)].reshape(JA * 16, 128)
            for x2 in range(X // 2):
                rhs = jnp.concatenate([pair_of(x2)] * 4, axis=0)
                o = jnp.dot(lhs, rhs, preferred_element_type=f32).astype(bf16)
                for j in range(JA):
                    for e in range(2):
                        abuf[2 * x2 + e, :, pl.ds((c * JA + j) * K, K)] = (
                            o[j * 16 : j * 16 + 16, e * K : e * K + K])

    def left_sums(h):
        for c in range(J // JA):
            j0 = c * JA
            rhs = jnp.concatenate([pb[j0 + j] for j in range(JA)], axis=1)
            lhs = abuf[:, :, pl.ds(j0 * K, JA * K)].reshape(X * 16, JA * K)
            o = lax.dot_general(lhs, rhs, NT, preferred_element_type=f32)
            for e in range(2):
                v = o[:, e * 128 : e * 128 + 128].reshape(X, 16, 128)
                if c == 0:
                    acc[h, e, :, pl.ds(0, 16), :] = v
                else:
                    acc[h, e, :, pl.ds(0, 16), :] += v

    def left_block(h, n):
        v = [acc[h, e, :, n, :] for e in range(2)]
        return jnp.concatenate(v, axis=1) * SCALE

    def exchange(h):
        return pltpu.make_async_remote_copy(
            lxs.at[h], lx.at[h], xs_sem.at[h], x_in.at[h], device_id=mate, device_id_type=MESH)

    def give_mate(h):
        @pl.when(core == 0)
        def _():
            for n in range(8):
                lxs[h, n] = left_block(h, 8 + n).astype(bf16)

        @pl.when(core == 1)
        def _():
            for n in range(8):
                lxs[h, n] = left_block(h, n).astype(bf16)

        exchange(h).start()

    def left_copy(h, n):
        s = row_peer(h, n % 4) * G + (n // 4) * 2 + core
        there = s // 2
        return s, pltpu.make_async_remote_copy(
            lsend.at[h, n], lr.at[(chip - there + CHIPS) % CHIPS], gs_sem, g_in,
            device_id=(row, s), device_id_type=MESH)

    def send_left(h):
        exchange(h).wait_recv()

        @pl.when(core == 0)
        def _():
            for n in range(8):
                lsend[h, n] = (left_block(h, n) + lx[h, n].astype(f32)).astype(bf16)

        @pl.when(core == 1)
        def _():
            for n in range(8):
                lsend[h, n] = (left_block(h, 8 + n) + lx[h, n].astype(f32)).astype(bf16)

        for n in range(8):
            s, copy = left_copy(h, n)

            @pl.when(s != col)
            def _():
                copy.start()

            @pl.when(s == col)
            def _():
                lr[0] = lsend[h, n]

    def relay(h):
        part = lin.at[pl.ds(h * 16 + core * 8, 8)]
        return pltpu.make_async_remote_copy(
            part, part, lrs_sem.at[h], lr_in.at[h], device_id=mate, device_id_type=MESH)

    def spread_left(h):
        for e in range(2):
            lst[e, :, pl.ds(0, X), :] = lin[pl.ds(h * 16, 16), :, pl.ds(e * 128, 128)].astype(f32)

        @pl.loop(0, X // 4)
        def _(q):
            for d in range(4):
                x = q * 4 + d
                v = [lst[e, :, x, :] for e in range(2)]
                lbuf[h, x] = jnp.concatenate(v, axis=1).astype(bf16)

    def times_left(h):
        @pl.loop(0, J // JA)
        def _(c):
            lhs = lbuf[h].reshape(X * 16, I)
            for j2 in range(JA // 2):
                j = c * JA + 2 * j2
                rhs = jnp.concatenate([pb[j], pb[j + 1]], axis=1)
                o = jnp.dot(lhs, rhs, preferred_element_type=f32).astype(bf16)
                for e in range(2):
                    ubuf[:, j + e] = o[:, e * K : e * K + K].reshape(X, 16, K)

    def right_sums(h):
        @pl.loop(0, J // JA)
        def _(c):
            t = jnp.zeros((JA * 16, Y), f32)
            for x2 in range(X // 2):
                lhs = [ubuf[2 * x2 + e, pl.ds(c * JA, JA)].reshape(JA * 16, K) for e in range(2)]
                t = t + lax.dot_general(
                    jnp.concatenate(lhs, axis=1), pair_of(x2), NT, preferred_element_type=f32)
            rt[pl.ds(c * JA, JA), pl.ds(0, 16), :] = (t * SCALE).reshape(JA, 16, Y)

    def right_copy_back(h, t):
        return pltpu.make_async_remote_copy(
            rsend.at[h * 4 + t], rr.at[h * 4 + (4 - t) % 4], hs_sem, h_in.at[h],
            device_id=(row_peer(h, t), col), device_id_type=MESH)

    def send_right(h):
        for t in range(4):
            v = [rt[:, (s4 % 2) * 8 + (s4 // 2) * 4 + t, :] for s4 in range(G)]
            v = jnp.concatenate(v, axis=1).astype(bf16)
            if h or t:
                rsend[h * 4 + t] = v
                right_copy_back(h, t).start()
            else:
                rr[0] = v

    pltpu.make_async_copy(pf, pf, psem).wait()

    @pl.loop(0, J // 8)
    def _(c):
        pb[pl.ds(c * 8, 8)] = pf[pl.ds(c * 8, 8)].astype(bf16)

    pltpu.make_async_copy(rin.at[pl.ds(1, 3)], rin.at[pl.ds(1, 3)], rr_in.at[0]).wait()
    spread_right(0)
    times_weight(0)
    left_sums(0)
    give_mate(0)
    pltpu.make_async_copy(rin.at[pl.ds(4, 4)], rin.at[pl.ds(4, 4)], rr_in.at[1]).wait()
    spread_right(1)
    times_weight(1)
    send_left(0)
    pltpu.make_async_copy(lin.at[pl.ds(0, 15)], lin.at[pl.ds(0, 15)], l_in).wait()
    relay(0).start()
    relay(1).start()
    left_sums(1)
    give_mate(1)

    relay(1).wait_recv()
    spread_left(1)
    relay(0).wait_recv()
    spread_left(0)
    send_left(1)
    times_left(1)
    right_sums(1)
    send_right(1)
    times_left(0)
    right_sums(0)
    send_right(0)

    pltpu.make_async_copy(lr.at[pl.ds(1, 15)], lr.at[pl.ds(1, 15)], g_in).wait()
    total = lr[0].astype(f32)
    for d in range(1, CHIPS):
        total = total + lr[d].astype(f32)
    left_out[0] = total
    pltpu.make_async_copy(rr.at[pl.ds(4, 4)], rr.at[pl.ds(4, 4)], h_in.at[1]).wait()
    pltpu.make_async_copy(rr.at[pl.ds(1, 3)], rr.at[pl.ds(1, 3)], h_in.at[0]).wait()
    total = rr[0].astype(f32)
    for d in range(1, ROWS):
        total = total + rr[d].astype(f32)
    right_out[...] = jnp.transpose(total).reshape(G, Y, J)

    pltpu.make_async_copy(rin.at[pl.ds(0, 7)], rin.at[pl.ds(0, 7)], rs_sem).wait()
    pltpu.make_async_copy(lin.at[pl.ds(0, 15)], lin.at[pl.ds(0, 15)], ls_sem).wait()
    for h in range(2):
        relay(h).wait_send()
        exchange(h).wait_send()
    pltpu.make_async_copy(lr.at[pl.ds(0, 15)], lr.at[pl.ds(0, 15)], gs_sem).wait()
    pltpu.make_async_copy(rr.at[pl.ds(0, 7)], rr.at[pl.ds(0, 7)], hs_sem).wait()


def body(pair_grad, out_weight, left_factor, right_factor):
    vmem = pl.BlockSpec(memory_space=pltpu.VMEM)
    hbm = pl.BlockSpec(memory_space=pl.ANY)
    dma = pltpu.SemaphoreType.DMA
    return pl.pallas_call(
        kernel,
        out_shape=(
            jax.ShapeDtypeStruct((1, X, I), f32),
            jax.ShapeDtypeStruct((G, Y, J), f32),
        ),
        in_specs=[hbm, vmem, hbm, vmem],
        out_specs=(vmem, vmem),
        scratch_shapes=[
            pltpu.VMEM((J, I, K), f32),
            pltpu.VMEM((J, I, K), bf16),
            pltpu.VMEM((X, 16, J * K), bf16),
            pltpu.VMEM((X, J, 16, K), bf16),
            pltpu.VMEM((J, 128), bf16),
            pltpu.VMEM((ROWS, J, 128), bf16),
            pltpu.VMEM((ROWS, J, 128), f32),
            pltpu.VMEM((2, J, 16, 128), bf16),
            pltpu.VMEM((S, X, I), bf16),
            pltpu.VMEM((2, 16, 40, 128), f32),
            pltpu.VMEM((2, X, 16, I), bf16),
            pltpu.VMEM((2, 2, X, 24, 128), f32),
            pltpu.VMEM((2, 8, X, I), bf16),
            pltpu.VMEM((2, 8, X, I), bf16),
            pltpu.VMEM((2, 8, X, I), bf16),
            pltpu.VMEM((CHIPS, X, I), bf16),
            pltpu.VMEM((J, 24, Y), f32),
            pltpu.VMEM((ROWS, J, 128), bf16),
            pltpu.VMEM((ROWS, J, 128), bf16),
            dma, dma, dma, dma((2,)), dma, dma, dma((2,)), dma((2,)),
            dma((2,)), dma((2,)), dma, dma, dma, dma((2,)),
        ],
        compiler_params=pltpu.CompilerParams(
            collective_id=0, has_side_effects=True, vmem_limit_bytes=60 * 2**20),
        name="outer_product_mean_backward",
    )(pair_grad, out_weight, left_factor, right_factor)


def solution(mesh):
    placed = (P("row", "col", None), P(), P("col", None, "row"), P("row", None, "col"))
    return jax.shard_map(
        body,
        mesh=mesh,
        in_specs=placed,
        out_specs=(P("col", None, "row"), P("row", None, "col")),
        check_vma=False,
    )
```

time: 124 us -> 50.6 us (0.41)
  matrix products: 55.5 us -> 0 us
  Pallas kernels: 0 us -> 46.9 us
  starting transfers between devices: 32.8 us -> 0 us
  waiting for transfers between devices: 18.8 us -> 0 us
  other arithmetic: 7.92 us -> 0 us
  local copies, waits for them, and re-layouts: 7.32 us -> 2.85 us
    dot_general x3 -> x0, matrix products: 55.5 us -> none  [the longest x1 26.2 us: body(): jnp.einsum('ijk,xyk->ijxy', pair_low, grid, preferred_element_type=jnp.fl...]
    pallas_call x0 -> x1, Pallas kernels: none -> 46.9 us  [body(): pl.pallas_call(kernel, out_shape=(jax.ShapeDtypeStruct((1, X, I), f32), j...]
    all_to_all x4 -> x0, starting transfers between devices: 32.8 us -> none  [the longest x2 19.6 us: from_everyone(): lax.all_to_all(jnp.broadcast_to(shard[None], (size, *shard.shape)), axis,...]
    all_to_all x4 -> x0, waiting for transfers between devices: 18.8 us -> none  [the longest x2 15.9 us: summed_on_arrival(): blocks = lax.all_to_all(split_up(shard, dim, size), axis, 0, 0, tiled=True)]
    convert_element_type x1 -> x0, other arithmetic: 6.54 us -> none  [body(): pair_low = pair_grad.astype(jnp.bfloat16)]
    broadcast_in_dim x1 -> x0, local copies, waits for them, and re-layouts: 1.57 us -> none  [from_everyone(): jnp.broadcast_to(shard[None], (size, *shard.shape))]
    reduce_sum x2 -> x0, other arithmetic: 1.38 us -> none  [summed_on_arrival(): return jnp.sum(blocks.astype(jnp.float32), axis=0)]
    unnamed x8 -> x2, local copies, waits for them, and re-layouts: 3.09 us -> 2.85 us
  transfers between devices with their start and end apart: 4 -> 0, of which waited for: 2 -> 0; matrix products, arithmetic and copies ran while one was open for 41% -> 0% of each run, Pallas kernels for 0% -> 0%
where the time goes in v1:
time: 50.6 us; the launch traced here: 50.4 us
  Pallas kernels  46.9 us (93%)
  local copies, waits for them, and re-layouts  2.85 us (6%)
  between operations  0.64 us (1%)
    pallas_call x1, Pallas kernels, body(): pl.pallas_call(kernel, out_shape=(jax.ShapeDtypeStruct((1, X, I), f32), j...  46.9 us
    unnamed x2, local copies, waits for them, and re-layouts  2.85 us

profile of v1, /device:TPU:1, one launch (start us, length us, event | category | flops | bytes accessed | tf_op | source)
XLA Modules:
  0.0 50.4 jit_solution(3169862019008950556)
XLA Ops:
  0.6 46.9 %outer_product_mean_backward.1 = (f32[1,32,256]{2,1,0:T(8,128)}, f32[4,32,64]{2,1,0:T(8,128)}) custom-call(f32[256,64,128]{2,1,0:T(8,128)} %pair.1, bf16[1024,128]{1,0:T(8,128)(2,1)} %weight.1, bf16[1,32,256]{2,1,0:T(8,128)(2,1)} %left.1, bf16[4,32,64]{2,1,0:T(8,128)(2,1)} %right.1), custom_call_target="tpu_custom_call" | custom-call | tf_op jit(solution)/shard_map/outer_product_mean_backward/pallas_call | solution.py:291
  47.5 1.4 %copy.8 = f32[1,32,256]{2,1,0:T(8,128)} copy(f32[1,32,256]{2,1,0:T(8,128)} %get-tuple-element.4) | data formatting | bytes 65536
  48.9 1.5 %copy.9 = f32[4,32,64]{2,1,0:T(8,128)} copy(f32[4,32,64]{2,1,0:T(8,128)} %get-tuple-element.5) | data formatting | bytes 65536

commit v2 on v1

--- a/solution.py
+++ b/solution.py
@@ -12,19 +12,21 @@
 I, J, K, X, Y, S = 256, 64, 128, 32, 32, 32
 ROWS, COLS, CHIPS = 8, 32, 16
 G = 4
-JA = 16
+JA, JB = 16, 32
 SCALE = 1.0 / S
+VMEM_LIMIT = 57 * 2**20
 
 
 def kernel(
-    pair, weight, left, right,
+    pair, wsrc, left, rsrc,
     left_out, right_out,
-    pf, pb, abuf, ubuf,
+    weight, right, pf, pb, buf,
     rmine, rin, rst, rbuf,
     lin, lst, lbuf,
     acc, lxs, lx, lsend, lr,
     rt, rsend, rr,
-    psem, osem, rs_sem, rr_in, ls_sem, l_in, lrs_sem, lr_in,
+    left_sum, right_sum, done,
+    psem, osem, wsem, rsem, rs_sem, rr_in, ls_sem, l_in, lrs_sem, lr_in,
     xs_sem, x_in, gs_sem, g_in, hs_sem, h_in,
 ):
     row, col = lax.axis_index("row"), lax.axis_index("col")
@@ -44,15 +46,8 @@
 
     mine = slot_of(col)
 
-    own = pltpu.make_async_copy(left.at[0], lin.at[mine], osem)
-    own.start()
-
-    @pl.loop(0, I)
-    def _(i):
-        pltpu.make_async_copy(pair.at[i], pf.at[:, i, :], psem).start()
-
     barrier = pltpu.get_barrier_semaphore()
-    for h in range(2):
+    for h in (1, 0):
         for t in range(4):
             if h or t:
                 pl.semaphore_signal(barrier, inc=1, device_id=(row_peer(h, t), col), device_id_type=MESH)
@@ -62,6 +57,18 @@
     def _(d):
         pl.semaphore_signal(barrier, inc=1, device_id=(row, chip_peer(d)), device_id_type=MESH)
 
+    own = pltpu.make_async_copy(left.at[0], lin.at[mine], osem)
+    own.start()
+    rload = pltpu.make_async_copy(rsrc, right, rsem)
+    rload.start()
+    wload = pltpu.make_async_copy(wsrc, weight, wsem)
+    wload.start()
+
+    @pl.loop(0, I)
+    def _(i):
+        pltpu.make_async_copy(pair.at[i], pf.at[:, i, :], psem).start()
+
+    rload.wait()
     flipped = jnp.transpose(right[...].reshape(G * Y, J).astype(f32)).astype(bf16)
     rmine[...] = flipped
     rin[0] = flipped
@@ -102,29 +109,22 @@
         return jnp.concatenate([a, b], axis=1)
 
     def times_weight(h):
-        @pl.loop(0, J // JA)
+        @pl.loop(0, J // JB)
         def _(c):
-            lhs = rbuf[h, pl.ds(c * JA, JA)].reshape(JA * 16, 128)
+            lhs = rbuf[h, pl.ds(c * JB, JB)].reshape(JB * 16, 128)
             for x2 in range(X // 2):
                 rhs = jnp.concatenate([pair_of(x2)] * 4, axis=0)
                 o = jnp.dot(lhs, rhs, preferred_element_type=f32).astype(bf16)
-                for j in range(JA):
+                for j in range(JB):
                     for e in range(2):
-                        abuf[2 * x2 + e, :, pl.ds((c * JA + j) * K, K)] = (
-                            o[j * 16 : j * 16 + 16, e * K : e * K + K])
+                        buf[2 * x2 + e, c * JB + j] = o[j * 16 : j * 16 + 16, e * K : e * K + K]
 
     def left_sums(h):
-        for c in range(J // JA):
-            j0 = c * JA
-            rhs = jnp.concatenate([pb[j0 + j] for j in range(JA)], axis=1)
-            lhs = abuf[:, :, pl.ds(j0 * K, JA * K)].reshape(X * 16, JA * K)
-            o = lax.dot_general(lhs, rhs, NT, preferred_element_type=f32)
-            for e in range(2):
-                v = o[:, e * 128 : e * 128 + 128].reshape(X, 16, 128)
-                if c == 0:
-                    acc[h, e, :, pl.ds(0, 16), :] = v
-                else:
-                    acc[h, e, :, pl.ds(0, 16), :] += v
+        rhs = jnp.concatenate([pb[j] for j in range(J)], axis=1)
+        lhs = jnp.concatenate([buf[:, j].reshape(X * 16, K) for j in range(J)], axis=1)
+        o = lax.dot_general(lhs, rhs, NT, preferred_element_type=f32)
+        for e in range(2):
+            acc[h, e, :, pl.ds(0, 16), :] = o[:, e * 128 : e * 128 + 128].reshape(X, 16, 128)
 
     def left_block(h, n):
         v = [acc[h, e, :, n, :] for e in range(2)]
@@ -195,22 +195,21 @@
                 lbuf[h, x] = jnp.concatenate(v, axis=1).astype(bf16)
 
     def times_left(h):
-        @pl.loop(0, J // JA)
+        @pl.loop(0, J // JB)
         def _(c):
             lhs = lbuf[h].reshape(X * 16, I)
-            for j2 in range(JA // 2):
-                j = c * JA + 2 * j2
+            for j2 in range(JB // 2):
+                j = c * JB + 2 * j2
                 rhs = jnp.concatenate([pb[j], pb[j + 1]], axis=1)
                 o = jnp.dot(lhs, rhs, preferred_element_type=f32).astype(bf16)
                 for e in range(2):
-                    ubuf[:, j + e] = o[:, e * K : e * K + K].reshape(X, 16, K)
+                    buf[:, j + e] = o[:, e * K : e * K + K].reshape(X, 16, K)
 
     def right_sums(h):
-        @pl.loop(0, J // JA)
-        def _(c):
+        for c in range(J // JA):
             t = jnp.zeros((JA * 16, Y), f32)
             for x2 in range(X // 2):
-                lhs = [ubuf[2 * x2 + e, pl.ds(c * JA, JA)].reshape(JA * 16, K) for e in range(2)]
+                lhs = [buf[2 * x2 + e, pl.ds(c * JA, JA)].reshape(JA * 16, K) for e in range(2)]
                 t = t + lax.dot_general(
                     jnp.concatenate(lhs, axis=1), pair_of(x2), NT, preferred_element_type=f32)
             rt[pl.ds(c * JA, JA), pl.ds(0, 16), :] = (t * SCALE).reshape(JA, 16, Y)
@@ -230,6 +229,7 @@
             else:
                 rr[0] = v
 
+    wload.wait()
     pltpu.make_async_copy(pf, pf, psem).wait()
 
     @pl.loop(0, J // 8)
@@ -267,13 +267,17 @@
     total = lr[0].astype(f32)
     for d in range(1, CHIPS):
         total = total + lr[d].astype(f32)
-    left_out[0] = total
+    left_sum[0] = total
+    left_done = pltpu.make_async_copy(left_sum, left_out, done.at[0])
+    left_done.start()
     pltpu.make_async_copy(rr.at[pl.ds(4, 4)], rr.at[pl.ds(4, 4)], h_in.at[1]).wait()
     pltpu.make_async_copy(rr.at[pl.ds(1, 3)], rr.at[pl.ds(1, 3)], h_in.at[0]).wait()
     total = rr[0].astype(f32)
     for d in range(1, ROWS):
         total = total + rr[d].astype(f32)
-    right_out[...] = jnp.transpose(total).reshape(G, Y, J)
+    right_sum[...] = jnp.transpose(total).reshape(G, Y, J)
+    right_done = pltpu.make_async_copy(right_sum, right_out, done.at[1])
+    right_done.start()
 
     pltpu.make_async_copy(rin.at[pl.ds(0, 7)], rin.at[pl.ds(0, 7)], rs_sem).wait()
     pltpu.make_async_copy(lin.at[pl.ds(0, 15)], lin.at[pl.ds(0, 15)], ls_sem).wait()
@@ -282,24 +286,44 @@
         exchange(h).wait_send()
     pltpu.make_async_copy(lr.at[pl.ds(0, 15)], lr.at[pl.ds(0, 15)], gs_sem).wait()
     pltpu.make_async_copy(rr.at[pl.ds(0, 7)], rr.at[pl.ds(0, 7)], hs_sem).wait()
+    left_done.wait()
+    right_done.wait()
+
+
+def hand_over(left, right, left_out, right_out, left_in, right_in, sem):
+    loads = [
+        pltpu.make_async_copy(left, left_in, sem.at[0]),
+        pltpu.make_async_copy(right, right_in, sem.at[1]),
+    ]
+    stores = [
+        pltpu.make_async_copy(left_in, left_out, sem.at[2]),
+        pltpu.make_async_copy(right_in, right_out, sem.at[3]),
+    ]
+    for load in loads:
+        load.start()
+    for load, store in zip(loads, stores):
+        load.wait()
+        store.start()
+    for store in stores:
+        store.wait()
 
 
 def body(pair_grad, out_weight, left_factor, right_factor):
-    vmem = pl.BlockSpec(memory_space=pltpu.VMEM)
-    hbm = pl.BlockSpec(memory_space=pl.ANY)
+    hbm = pl.BlockSpec(memory_space=pltpu.HBM)
     dma = pltpu.SemaphoreType.DMA
-    return pl.pallas_call(
+    sums = pl.pallas_call(
         kernel,
         out_shape=(
             jax.ShapeDtypeStruct((1, X, I), f32),
             jax.ShapeDtypeStruct((G, Y, J), f32),
         ),
-        in_specs=[hbm, vmem, hbm, vmem],
-        out_specs=(vmem, vmem),
+        in_specs=[hbm] * 4,
+        out_specs=(hbm, hbm),
         scratch_shapes=[
+            pltpu.VMEM((X * Y, K), bf16),
+            pltpu.VMEM((G, Y, J), bf16),
             pltpu.VMEM((J, I, K), f32),
             pltpu.VMEM((J, I, K), bf16),
-            pltpu.VMEM((X, 16, J * K), bf16),
             pltpu.VMEM((X, J, 16, K), bf16),
             pltpu.VMEM((J, 128), bf16),
             pltpu.VMEM((ROWS, J, 128), bf16),
@@ -316,13 +340,31 @@
             pltpu.VMEM((J, 24, Y), f32),
             pltpu.VMEM((ROWS, J, 128), bf16),
             pltpu.VMEM((ROWS, J, 128), bf16),
-            dma, dma, dma, dma((2,)), dma, dma, dma((2,)), dma((2,)),
+            pltpu.VMEM((1, X, I), f32),
+            pltpu.VMEM((G, Y, J), f32),
+            dma((2,)),
+            dma, dma, dma, dma, dma, dma((2,)), dma, dma, dma((2,)), dma((2,)),
             dma((2,)), dma((2,)), dma, dma, dma, dma((2,)),
         ],
         compiler_params=pltpu.CompilerParams(
-            collective_id=0, has_side_effects=True, vmem_limit_bytes=60 * 2**20),
+            collective_id=0, has_side_effects=True, vmem_limit_bytes=VMEM_LIMIT),
         name="outer_product_mean_backward",
     )(pair_grad, out_weight, left_factor, right_factor)
+    return pl.pallas_call(
+        hand_over,
+        out_shape=(
+            jax.ShapeDtypeStruct((1, X, I), f32),
+            jax.ShapeDtypeStruct((G, Y, J), f32),
+        ),
+        in_specs=[hbm, hbm],
+        out_specs=(hbm, hbm),
+        scratch_shapes=[
+            pltpu.VMEM((1, X, I), f32),
+            pltpu.VMEM((G, Y, J), f32),
+            dma((4,)),
+        ],
+        name="hand_over",
+    )(*sums)
 
 
 def solution(mesh):

time: 50.6 us -> 44.3 us (0.88)
  Pallas kernels: 46.9 us -> 43.3 us
  local copies, waits for them, and re-layouts: 2.85 us -> 0 us
    pallas_call x1, Pallas kernels: 46.9 us -> 41.8 us  [body(): pl.pallas_call(kernel, out_shape=(jax.ShapeDtypeStruct((1, X, I), f32), j...]
    unnamed x2 -> x0, local copies, waits for them, and re-layouts: 2.85 us -> none
    pallas_call x0 -> x1, Pallas kernels: none -> 1.52 us  [body(): pl.pallas_call(hand_over, out_shape=(jax.ShapeDtypeStruct((1, X, I), f32)...]
where the time goes in v2:
time: 44.3 us; the launch traced here: 44.1 us
  Pallas kernels  43.3 us (98%)
  between operations  0.8 us (2%)
    pallas_call x1, Pallas kernels, body(): pl.pallas_call(kernel, out_shape=(jax.ShapeDtypeStruct((1, X, I), f32), j...  41.8 us
    pallas_call x1, Pallas kernels, body(): pl.pallas_call(hand_over, out_shape=(jax.ShapeDtypeStruct((1, X, I), f32)...  1.52 us

profile of v2, /device:TPU:1, one launch (start us, length us, event | category | flops | bytes accessed | tf_op | source)
XLA Modules:
  0.0 44.1 jit_solution(6246773387020899540)
XLA Ops:
  0.6 41.8 %outer_product_mean_backward.1 = (f32[1,32,256]{2,1,0:T(8,128)}, f32[4,32,64]{2,1,0:T(8,128)}) custom-call(f32[256,64,128]{2,1,0:T(8,128)} %pair.1, bf16[1024,128]{1,0:T(8,128)(2,1)} %wsrc.1, bf16[1,32,256]{2,1,0:T(8,128)(2,1)} %left.1, bf16[4,32,64]{2,1,0:T(8,128)(2,1)} %rsrc.1), custom_call_target="tpu_custom_call" | custom-call | tf_op jit(solution)/shard_map/outer_product_mean_backward/pallas_call | solution.py:314
  42.5 1.5 %hand_over.1 = (f32[1,32,256]{2,1,0:T(8,128)}, f32[4,32,64]{2,1,0:T(8,128)}) custom-call(f32[1,32,256]{2,1,0:T(8,128)} %get-tuple-element.4.left, f32[4,32,64]{2,1,0:T(8,128)} %get-tuple-element.5.right), custom_call_target="tpu_custom_call" | custom-call | tf_op jit(solution)/shard_map/hand_over/pallas_call | solution.py:353

commit v3 on v2

--- a/solution.py
+++ b/solution.py
@@ -80,7 +80,7 @@
             rmine, rin.at[h * 4 + (4 - t) % 4], rs_sem, rr_in.at[h],
             device_id=(row_peer(h, t), col), device_id_type=MESH)
 
-    for h in (1, 0):
+    for h in (0, 1):
         for t in range(4):
             if h or t:
                 right_copy(h, t).start()
@@ -244,10 +244,10 @@
     pltpu.make_async_copy(rin.at[pl.ds(4, 4)], rin.at[pl.ds(4, 4)], rr_in.at[1]).wait()
     spread_right(1)
     times_weight(1)
+    pltpu.make_async_copy(lin.at[pl.ds(0, 15)], lin.at[pl.ds(0, 15)], l_in).wait()
+    relay(1).start()
+    relay(0).start()
     send_left(0)
-    pltpu.make_async_copy(lin.at[pl.ds(0, 15)], lin.at[pl.ds(0, 15)], l_in).wait()
-    relay(0).start()
-    relay(1).start()
     left_sums(1)
     give_mate(1)
 

time: 44.3 us -> 44.3 us (level)
  no operation moved by 1% of the time
where the time goes in v3:
time: 44.3 us; the launch traced here: 44.1 us
  Pallas kernels  43.3 us (98%)
  between operations  0.8 us (2%)
    pallas_call x1, Pallas kernels, body(): pl.pallas_call(kernel, out_shape=(jax.ShapeDtypeStruct((1, X, I), f32), j...  41.8 us
    pallas_call x1, Pallas kernels, body(): pl.pallas_call(hand_over, out_shape=(jax.ShapeDtypeStruct((1, X, I), f32)...  1.52 us

profile of v3, /device:TPU:1, one launch (start us, length us, event | category | flops | bytes accessed | tf_op | source)
XLA Modules:
  0.0 44.1 jit_solution(17882313524803078112)
XLA Ops:
  0.6 41.8 %outer_product_mean_backward.1 = (f32[1,32,256]{2,1,0:T(8,128)}, f32[4,32,64]{2,1,0:T(8,128)}) custom-call(f32[256,64,128]{2,1,0:T(8,128)} %pair.1, bf16[1024,128]{1,0:T(8,128)(2,1)} %wsrc.1, bf16[1,32,256]{2,1,0:T(8,128)(2,1)} %left.1, bf16[4,32,64]{2,1,0:T(8,128)(2,1)} %rsrc.1), custom_call_target="tpu_custom_call" | custom-call | tf_op jit(solution)/shard_map/outer_product_mean_backward/pallas_call | solution.py:314
  42.5 1.5 %hand_over.1 = (f32[1,32,256]{2,1,0:T(8,128)}, f32[4,32,64]{2,1,0:T(8,128)}) custom-call(f32[1,32,256]{2,1,0:T(8,128)} %get-tuple-element.4.left, f32[4,32,64]{2,1,0:T(8,128)} %get-tuple-element.5.right), custom_call_target="tpu_custom_call" | custom-call | tf_op jit(solution)/shard_map/hand_over/pallas_call | solution.py:353
